TPU v7x, 256 devices: a whole 4x4x8 slice. The times are simulated.
256 devices in a mesh: grp: 4 (over z_lo), mem: 64 (over x, z_hi, y, core).
Axes of the slice: x: 4, y: 4, z: 8 (z_hi: 2, z_lo: 4; z = z_hi * 4 + z_lo), core: 2. Of those that a mesh axis runs over, the one named last changes fastest.
Arguments:
- embeddings: bfloat16 [262144, 4096], P(('grp', 'mem')), may hold values from -6 to 6
- local_picks: int32 [4, 512], P('grp', 'mem'), may hold values from 0 to 1023
- second_picks: int32 [4, 16], P('grp'), may hold values from 0 to 511
- final_picks: int32 [16], replicated, may hold values from 0 to 63
Outputs:
- gain_table: float32 [64, 512], P('grp', 'mem')
- final_cover: float32 [262144], P(('grp', 'mem'))
Inputs may be any that keep to these rules, and one draw needn't show every extreme that they name: `local_picks`: entry (g, m * 8 + k) names a row among the 1024 points of device m of group g; repeats may occur. `second_picks`: candidate indices of the group, in greedy order; repeats may occur. `final_picks`: index g * 16 + t names group g's second-round pick t; repeats may occur.
All inputs are finite; a program needn't handle non-finite values.
Results may differ from a plain program's by a relative error of at most 0.0003.
Values may be sent and summed in bfloat16 or wider, within the bound.
A program may use at most 64 MiB of HBM per device.

v0:
```python
import jax
import jax.numpy as jnp
from jax import lax
from jax.sharding import PartitionSpec as P

D = 4096


def split_up(x, dim, size):
    before, after = (x.shape[:dim], x.shape[dim + 1 :])
    return jnp.moveaxis(x.reshape(*before, size, -1, *after), dim, 0)


def sent_and_summed(x, axis, dim):
    parts = split_up(x, dim, lax.axis_size(axis))
    arrived = lax.all_to_all(parts, axis, split_axis=0, concat_axis=0, tiled=True)
    return arrived.sum(axis=0)


def per_device(embeddings, local_picks, second_picks, final_picks):
    scaling = float(D) ** (-0.5)
    point_count = embeddings.shape[0]
    local_count = local_picks.shape[1]
    second_list = second_picks[0]
    rounds = second_list.shape[0]
    member = lax.axis_index("mem")
    choose = (local_picks[0][:, None] == lax.iota(jnp.int32, point_count)[None, :]).astype(
        jnp.bfloat16
    )
    own_rows = jnp.dot(choose, embeddings, preferred_element_type=jnp.float32).astype(jnp.bfloat16)

    def similar(other_rows):
        dims = (((1,), (1,)), ((), ()))
        return (
            lax.dot_general(embeddings, other_rows, dims, preferred_element_type=jnp.float32)
            * scaling
        )

    similar_map = similar(lax.all_gather(own_rows, "mem", axis=0, tiled=True))
    group_index = lax.axis_index("grp")
    wanted_group = final_picks // rounds
    winner_slot = final_picks % rounds
    cand_index = jnp.take(second_list, winner_slot)
    owned = (wanted_group == group_index) & (cand_index // local_count == member)
    local_slot = cand_index - member * local_count
    select_table = (
        (local_slot[:, None] == lax.iota(jnp.int32, local_count)[None, :]) & owned[:, None]
    ).astype(jnp.bfloat16)
    row_terms = jnp.dot(select_table, own_rows, preferred_element_type=jnp.float32)
    final_rows = lax.psum(row_terms, ("grp", "mem")).astype(jnp.bfloat16)
    own_block = lax.dynamic_slice_in_dim(similar_map, member * local_count, local_count, 1)
    coverage = jnp.max(own_block, axis=1)
    chosen_cols = jnp.take(similar_map, second_list, axis=1)

    def greedy_step(cover_now, column):
        partial_value = jnp.sum(jnp.maximum(similar_map - cover_now[:, None], 0.0), axis=0)
        return (jnp.maximum(cover_now, column), partial_value)

    _, partials = lax.scan(greedy_step, coverage, chosen_cols.T)
    gain_table = sent_and_summed(partials, "mem", 1) / point_count
    final_cover = jnp.max(similar(final_rows), axis=1)
    return (gain_table, final_cover)


def solution(mesh):
    placed = (P(("grp", "mem"), None), P("grp", "mem"), P("grp", None), P())
    return jax.shard_map(
        per_device,
        mesh=mesh,
        in_specs=placed,
        out_specs=(P("grp", "mem"), P(("grp", "mem"))),
        check_vma=False,
    )
```

profile of v0, /device:TPU:1, one launch (start us, length us, event | category | flops | bytes accessed | tf_op | source)
XLA Modules:
  0.0 156.5 jit_solution(1627441644940368098)
XLA Ops:
  7.2 5.3 %convolution_convert_fusion = bf16[8,4096]{1,0:T(8,128)(2,1)} fusion(bf16[1024,4096]{1,0:T(8,128)(2,1)} %param.6, s32[8]{0:T(128)} %bitcast.33), kind=kOutput, calls=%fused_computation.4 | convolution fusion | flops 67149824 | bytes 8454176 | tf_op jit(solution)/shard_map/dot_general | solution.py:30
  12.6 0.7 gather_fusion.1
  13.3 1.1 fusion.4
  14.4 85.0 %all-reduce.1 = bf16[16,4096]{1,0:T(8,128)(2,1)S(1)} all-reduce(f32[16,4096]{1,0:T(8,128)S(1)} %fusion.4), channel_id=1, replica_groups=mesh['grp'=4,'mem'=64] {'grp','mem'}, use_global_device_ids=true, to_apply=%region_5.6 | all-reduce | flops 65536 | bytes 393216 | tf_op jit(solution)/shard_map/psum | solution.py:50
  99.5 10.2 %all-gather.2.cloned.1.call-done = bf16[512,4096]{1,0:T(8,128)(2,1)} async-done(((bf16[8,4096]{1,0:T(8,128)(2,1)}), bf16[512,4096]{1,0:T(8,128)(2,1)}) %all-gather.2.cloned.1.call-update) | async-done | bytes 4194320 | tf_op jit(solution)/shard_map/all_gather | solution.py:39
  109.7 8.2 %convolution_multiply_fusion = f32[512,1024]{1,0:T(8,128)S(1)} fusion(bf16[512,4096]{1,0:T(8,128)(2,1)} %all-gather.2.cloned.1.call-done, bf16[1024,4096]{1,0:T(8,128)(2,1)} %param.6), kind=kOutput, calls=%fused_computation.5 | convolution fusion | flops 4295491584 | bytes 14680064 | tf_op jit(solution)/shard_map/dot_general | solution.py:35
  117.9 1.3 copy-done.1
  119.2 1.9 %copy.7 = f32[1024,512]{1,0:T(8,128)S(1)} copy(f32[1024,512]{0,1:T(8,128)} %bitcast.29) | data formatting | bytes 4194304 | tf_op jit(solution)/shard_map/while | solution.py:59
  121.2 2.2 %gather_fusion = f32[16,1024]{1,0:T(8,128)S(1)} fusion(f32[1024,512]{0,1:T(8,128)} %bitcast.30, s32[1024]{0:T(1024)S(1)} %pad_clamp_fusion.1), kind=kCustom, calls=%fused_computation | custom fusion | bytes 131136 | tf_op jit(solution)/shard_map/jit(_take)/gather | solution.py:53
  123.4 0.1 broadcast_select_fusion
  123.5 6.4 %while.12 = (s32[]{:T(128)}, f32[1024]{0:T(1024)S(1)}, f32[16,512]{1,0:T(8,128)S(1)}, f32[16,1024]{1,0:T(8,128)S(1)}, f32[1024,512]{1,0:T(8,128)S(1)}, /*index=5*/s32[]{:T(128)}, s32[]{:T(128)}) while((s32[]{:T(128)}, f32[1024]{0:T(1024)S(1)}, f32[16,512]{1,0:T(8,128)S(1)}, f32[16,1024]{1,0:T(8,128)S(1)}, f32[1024,512]{1,0:T(8,128)S(1)}, ...), condition=%wide.region_3.4_spmd, body=%wide.region_1.3_spmd.sunk | while | flops 1573378 | bytes 2127965 | solution.py:59
  123.5 0.3 maximum_reduce_fusion.2
  123.8 0.1 dynamic_update_slice.5
  123.9 0.3 maximum_reduce_fusion.2
  124.2 0.1 dynamic_update_slice.5
  124.3 0.3 maximum_reduce_fusion.2
  124.6 0.1 dynamic_update_slice.5
  124.7 0.3 maximum_reduce_fusion.2
  125.0 0.1 dynamic_update_slice.5
  125.1 0.3 maximum_reduce_fusion.2
  125.5 0.3 maximum_reduce_fusion.2
  125.8 0.1 dynamic_update_slice.5
  125.9 0.3 maximum_reduce_fusion.2
  126.2 0.1 dynamic_update_slice.5
  126.3 0.3 maximum_reduce_fusion.2
  126.7 0.3 maximum_reduce_fusion.2
  127.0 0.1 dynamic_update_slice.5
  127.1 0.3 maximum_reduce_fusion.2
  127.4 0.1 dynamic_update_slice.5
  127.5 0.3 maximum_reduce_fusion.2
  127.8 0.1 dynamic_update_slice.5
  127.9 0.3 maximum_reduce_fusion.2
  128.3 0.3 maximum_reduce_fusion.2
  128.6 0.1 dynamic_update_slice.5
  128.7 0.3 maximum_reduce_fusion.2
  129.0 0.1 dynamic_update_slice.5
  129.1 0.3 maximum_reduce_fusion.2
  129.5 0.3 maximum_reduce_fusion.2
  129.9 0.1 copy.8
  130.0 0.8 reshape.71
  130.8 5.1 %all-to-all-start = ((f32[64,1,128]{2,1,0:T(1,128)}), f32[64,1,128]{2,1,0:T(1,128)S(1)}, u32[]{:S(2)}, u32[]{:S(2)}) async-start(f32[64,1,128]{2,1,0:T(1,128)} %reshape.71), calls=%async_computation | async-start | bytes 65536 | tf_op jit(solution)/shard_map/all_to_all | solution.py:16
  135.9 6.3 %fusion = f32[1024]{0:T(1024)} fusion(bf16[1024,4096]{1,0:T(8,128)(2,1)} %param.6, bf16[16,4096]{1,0:T(8,128)(2,1)S(1)} %all-reduce.1), kind=kOutput, calls=%fused_computation.7 | convolution fusion | flops 134249472 | bytes 8523776 | tf_op jit(solution)/shard_map/dot_general | solution.py:35
  142.1 5.5 %all-to-all-done = f32[64,1,128]{2,1,0:T(1,128)S(1)} async-done(((f32[64,1,128]{2,1,0:T(1,128)}), f32[64,1,128]{2,1,0:T(1,128)S(1)}, u32[]{:S(2)}, u32[]{:S(2)}) %all-to-all-start) | async-done | bytes 32800 | tf_op jit(solution)/shard_map/all_to_all | solution.py:16
  147.6 0.5 broadcast.98
  148.1 0.7 reduce.2
  148.8 0.1 reshape.72
  149.0 0.1 bitcast_reduce_fusion
  149.0 0.6 broadcast_multiply_fusion
  (54 shorter events, 0.7 us)
Async XLA Ops:
  7.2 102.5 %all-gather.2.cloned.1.call-start = ((), (), s32[]{:S(2)}) async-start(), calls=%async_computation.1 | async-start | bytes 4259840 | tf_op jit(solution)/shard_map/all_gather | solution.py:39
  7.2 5.3 %copy-start.2 = (s32[16]{0:T(128)S(1)}, s32[16]{0:T(128)}, u32[]{:S(2)}) copy-start(s32[16]{0:T(128)} %param.9) | copy-start | bytes 196
  7.2 5.4 %copy-start = (s32[1,16]{1,0:T(1,128)S(1)}, s32[1,16]{1,0:T(1,128)}, u32[]{:S(2)}) copy-start(s32[1,16]{1,0:T(1,128)} %param.8) | copy-start | bytes 196
  117.9 1.4 copy-start.1
  130.8 16.8 %all-to-all-start = ((f32[64,1,128]{2,1,0:T(1,128)}), f32[64,1,128]{2,1,0:T(1,128)S(1)}, u32[]{:S(2)}, u32[]{:S(2)}) async-start(f32[64,1,128]{2,1,0:T(1,128)} %reshape.71), calls=%async_computation | async-start | bytes 65536 | tf_op jit(solution)/shard_map/all_to_all | solution.py:16
Sparse Core Ops, SparseCore 0:
  12.7 96.9 all-gather.1
where the time goes:
time: 157 us; the launch traced here: 156 us
  blocking collectives  85 us (54%)
  matrix products  20.8 us (13%)
  waiting for transfers between devices  15.7 us (10%)
  between operations  14.2 us (9%)
  local copies, waits for them, and re-layouts  8.8 us (6%)
  other arithmetic  6.21 us (4%)
  starting transfers between devices  5.12 us (3%)
    psum x1, blocking collectives, per_device(): final_rows = lax.psum(row_terms, ('grp', 'mem')).astype(jnp.bfloat16)  85 us
    dot_general x2, matrix products, similar(): lax.dot_general(embeddings, other_rows, dims, preferred_element_type=jnp....  14.5 us
    all_gather x1, waiting for transfers between devices, per_device(): similar_map = similar(lax.all_gather(own_rows, 'mem', axis=0, tiled=True))  10.2 us
    all_to_all x1, waiting for transfers between devices, sent_and_summed(): lax.all_to_all(parts, axis, split_axis=0, concat_axis=0, tiled=True)  5.46 us
    dot_general x1, matrix products, per_device(): jnp.dot(choose, embeddings, preferred_element_type=jnp.float32)  5.28 us
    all_to_all x1, starting transfers between devices, sent_and_summed(): lax.all_to_all(parts, axis, split_axis=0, concat_axis=0, tiled=True)  5.08 us
    reduce_sum x16, other arithmetic, greedy_step(): jnp.sum(jnp.maximum(similar_map - cover_now[:, None], 0.0), axis=0)  4.57 us
  transfers between devices with their start and end apart: 2, of which 2 were waited for; matrix products, arithmetic and copies ran while one was open for 5% of the time, Pallas kernels for 0%

commit v1 on v0

--- a/solution.py
+++ b/solution.py
@@ -36,7 +36,11 @@
             * scaling
         )
 
-    similar_map = similar(lax.all_gather(own_rows, "mem", axis=0, tiled=True))
+    similar_map = similar(
+        jnp.concatenate(
+            lax.all_to_all(jnp.stack([own_rows] * lax.axis_size("mem")), "mem", 0, 0), axis=0
+        )
+    )
     group_index = lax.axis_index("grp")
     wanted_group = final_picks // rounds
     winner_slot = final_picks % rounds

time: 157 us -> 206 us (1.31)
  blocking collectives: 85 us -> 139 us
  starting transfers between devices: 5.12 us -> 23.3 us
  between operations: 14.2 us -> 0.83 us
  waiting for transfers between devices: 15.7 us -> 5.46 us
  local copies, waits for them, and re-layouts: 8.8 us -> 11.3 us
    psum x1, blocking collectives: 85 us -> 139 us  [per_device(): final_rows = lax.psum(row_terms, ('grp', 'mem')).astype(jnp.bfloat16)]
    all_to_all x0 -> x1, starting transfers between devices: none -> 15.9 us  [per_device(): lax.all_to_all(jnp.stack([own_rows] * lax.axis_size('mem')), 'mem', 0, 0)]
    all_gather x1 -> x0, waiting for transfers between devices: 10.2 us -> none  [per_device(): similar_map = similar(lax.all_gather(own_rows, 'mem', axis=0, tiled=True))]
    another operation x0 -> x1, local copies, waits for them, and re-layouts: none -> 2.48 us  [per_device(): jnp.stack([own_rows] * lax.axis_size('mem'))]
    all_to_all x1, starting transfers between devices: 5.08 us -> 7.33 us  [sent_and_summed(): lax.all_to_all(parts, axis, split_axis=0, concat_axis=0, tiled=True)]
  transfers between devices with their start and end apart: 2 -> 2, of which waited for: 2 -> 1; matrix products, arithmetic and copies ran while one was open for 5% -> 4% of each run, Pallas kernels for 0% -> 0%
where the time goes in v1:
time: 206 us
  blocking collectives  139 us (67%)
  starting transfers between devices  23.3 us (11%)
  matrix products  19.4 us (9%)
  local copies, waits for them, and re-layouts  11.3 us (5%)
  other arithmetic  6.2 us (3%)
  waiting for transfers between devices  5.46 us (3%)
    psum x1, blocking collectives, per_device(): final_rows = lax.psum(row_terms, ('grp', 'mem')).astype(jnp.bfloat16)  139 us
    all_to_all x1, starting transfers between devices, per_device(): lax.all_to_all(jnp.stack([own_rows] * lax.axis_size('mem')), 'mem', 0, 0)  15.9 us
    dot_general x2, matrix products, similar(): lax.dot_general(embeddings, other_rows, dims, preferred_element_type=jnp....  14.5 us
    all_to_all x1, starting transfers between devices, sent_and_summed(): lax.all_to_all(parts, axis, split_axis=0, concat_axis=0, tiled=True)  7.33 us
    all_to_all x1, waiting for transfers between devices, sent_and_summed(): lax.all_to_all(parts, axis, split_axis=0, concat_axis=0, tiled=True)  5.46 us
    dot_general x1, matrix products, per_device(): jnp.dot(choose, embeddings, preferred_element_type=jnp.float32)  4.63 us
    reduce_sum x16, other arithmetic, greedy_step(): jnp.sum(jnp.maximum(similar_map - cover_now[:, None], 0.0), axis=0)  4.55 us
  transfers between devices with their start and end apart: 2, of which 1 were waited for; matrix products, arithmetic and copies ran while one was open for 4% of the time, Pallas kernels for 0%

profile of v1, /device:TPU:1, one launch (start us, length us, event | category | flops | bytes accessed | tf_op | source)
XLA Modules:
  0.0 205.9 jit_solution(7602057694090181483)
XLA Ops:
  0.6 4.6 %convolution_convert_fusion = bf16[8,4096]{1,0:T(8,128)(2,1)S(1)} fusion(bf16[1024,4096]{1,0:T(8,128)(2,1)} %param.6, s32[8]{0:T(128)} %bitcast.37), kind=kOutput, calls=%fused_computation.4 | convolution fusion | flops 67149824 | bytes 8454176 | tf_op jit(solution)/shard_map/dot_general | solution.py:30
  5.3 2.5 %stack.2 = bf16[64,8,4096]{2,1,0:T(8,128)(2,1)} broadcast(bf16[8,4096]{1,0:T(8,128)(2,1)S(1)} %convolution_convert_fusion), dimensions={1,2} | broadcast | bytes 4259840 | tf_op jit(solution)/shard_map/stack | solution.py:41
  7.7 15.9 %all-to-all-start = ((bf16[64,8,4096]{2,1,0:T(8,128)(2,1)}), bf16[64,8,4096]{2,1,0:T(8,128)(2,1)}, u32[]{:S(2)}, u32[]{:S(2)}) async-start(bf16[64,8,4096]{2,1,0:T(8,128)(2,1)} %stack.2), calls=%async_computation | async-start | bytes 8388608 | tf_op jit(solution)/shard_map/all_to_all | solution.py:41
  23.7 0.7 gather_fusion.1
  24.5 0.2 fusion.9
  24.7 138.9 %all-reduce.1 = bf16[16,4096]{1,0:T(8,128)(2,1)S(1)} all-reduce(f32[16,4096]{1,0:T(8,128)S(1)} %fusion.9), channel_id=1, replica_groups=mesh['grp'=4,'mem'=64] {'grp','mem'}, use_global_device_ids=true, to_apply=%region_5.6 | all-reduce | flops 65536 | bytes 393216 | tf_op jit(solution)/shard_map/psum | solution.py:54
  163.6 8.2 %fusion.2 = f32[512,1024]{1,0:T(8,128)S(1)} fusion(bf16[1024,4096]{1,0:T(8,128)(2,1)} %param.6, bf16[64,8,4096]{2,1,0:T(8,128)(2,1)} %all-to-all-done), kind=kOutput, calls=%fused_computation.7 | convolution fusion | flops 4295491584 | bytes 14680064 | tf_op jit(solution)/shard_map/dot_general | solution.py:35
  171.9 1.3 copy-done.1
  173.2 1.9 copy.7
  175.2 2.2 %gather_fusion = f32[16,1024]{1,0:T(8,128)S(1)} fusion(f32[1024,512]{0,1:T(8,128)} %bitcast.34, s32[1024]{0:T(1024)S(1)} %pad_clamp_fusion.1), kind=kCustom, calls=%fused_computation | custom fusion | bytes 131136 | tf_op jit(solution)/shard_map/jit(_take)/gather | solution.py:57
  177.4 0.1 broadcast_select_fusion
  177.5 6.4 %while.12 = (s32[]{:T(128)}, f32[1024]{0:T(1024)S(1)}, f32[16,512]{1,0:T(8,128)S(1)}, f32[16,1024]{1,0:T(8,128)S(1)}, f32[1024,512]{1,0:T(8,128)S(1)}, /*index=5*/s32[]{:T(128)}, s32[]{:T(128)}) while((s32[]{:T(128)}, f32[1024]{0:T(1024)S(1)}, f32[16,512]{1,0:T(8,128)S(1)}, f32[16,1024]{1,0:T(8,128)S(1)}, f32[1024,512]{1,0:T(8,128)S(1)}, ...), condition=%wide.region_3.4_spmd, body=%wide.region_1.3_spmd.sunk | while | flops 1573378 | bytes 2127965 | solution.py:63
  177.5 0.3 maximum_reduce_fusion.2
  177.8 0.1 dynamic_update_slice.5
  177.9 0.3 maximum_reduce_fusion.2
  178.2 0.1 dynamic_update_slice.5
  178.3 0.3 maximum_reduce_fusion.2
  178.6 0.1 dynamic_update_slice.5
  178.7 0.3 maximum_reduce_fusion.2
  179.0 0.1 dynamic_update_slice.5
  179.1 0.3 maximum_reduce_fusion.2
  179.5 0.3 maximum_reduce_fusion.2
  179.8 0.1 dynamic_update_slice.5
  179.9 0.3 maximum_reduce_fusion.2
  180.3 0.3 maximum_reduce_fusion.2
  180.7 0.3 maximum_reduce_fusion.2
  181.0 0.1 dynamic_update_slice.5
  181.1 0.3 maximum_reduce_fusion.2
  181.5 0.3 maximum_reduce_fusion.2
  181.8 0.1 dynamic_update_slice.5
  181.9 0.3 maximum_reduce_fusion.2
  182.2 0.1 dynamic_update_slice.5
  182.3 0.3 maximum_reduce_fusion.2
  182.7 0.3 maximum_reduce_fusion.2
  183.0 0.1 dynamic_update_slice.5
  183.1 0.3 maximum_reduce_fusion.2
  183.4 0.1 dynamic_update_slice.5
  183.5 0.3 maximum_reduce_fusion.2
  183.9 0.1 copy.8
  184.0 0.8 reshape.77
  184.8 7.3 %all-to-all-start.1 = ((f32[64,1,128]{2,1,0:T(1,128)}), f32[64,1,128]{2,1,0:T(1,128)S(1)}, u32[]{:S(2)}, u32[]{:S(2)}) async-start(f32[64,1,128]{2,1,0:T(1,128)} %reshape.77), calls=%async_computation.1 | async-start | bytes 65536 | tf_op jit(solution)/shard_map/all_to_all | solution.py:16
  192.1 6.3 %fusion.5 = f32[1024]{0:T(1024)} fusion(bf16[1024,4096]{1,0:T(8,128)(2,1)} %param.6, bf16[16,4096]{1,0:T(8,128)(2,1)S(1)} %all-reduce.1), kind=kOutput, calls=%fused_computation.9 | convolution fusion | flops 134249472 | bytes 8523776 | tf_op jit(solution)/shard_map/dot_general | solution.py:35
  198.4 5.5 %all-to-all-done.1 = f32[64,1,128]{2,1,0:T(1,128)S(1)} async-done(((f32[64,1,128]{2,1,0:T(1,128)}), f32[64,1,128]{2,1,0:T(1,128)S(1)}, u32[]{:S(2)}, u32[]{:S(2)}) %all-to-all-start.1) | async-done | bytes 32800 | tf_op jit(solution)/shard_map/all_to_all | solution.py:16
  203.8 0.5 broadcast.100
  204.3 0.7 reduce.2
  205.1 0.1 reshape.78
  205.2 0.1 bitcast_reduce_fusion
  205.3 0.6 broadcast_multiply_fusion
  (54 shorter events, 0.8 us)
Async XLA Ops:
  7.7 16.0 %copy-start.2 = (s32[16]{0:T(128)S(1)}, s32[16]{0:T(128)}, u32[]{:S(2)}) copy-start(s32[16]{0:T(128)} %param.9) | copy-start | bytes 196
  7.7 16.0 %copy-start = (s32[1,16]{1,0:T(1,128)S(1)}, s32[1,16]{1,0:T(1,128)}, u32[]{:S(2)}) copy-start(s32[1,16]{1,0:T(1,128)} %param.8) | copy-start | bytes 196
  7.7 155.9 %all-to-all-start = ((bf16[64,8,4096]{2,1,0:T(8,128)(2,1)}), bf16[64,8,4096]{2,1,0:T(8,128)(2,1)}, u32[]{:S(2)}, u32[]{:S(2)}) async-start(bf16[64,8,4096]{2,1,0:T(8,128)(2,1)} %stack.2), calls=%async_computation | async-start | bytes 8388608 | tf_op jit(solution)/shard_map/all_to_all | solution.py:41
  171.9 1.4 copy-start.1
  184.8 19.1 %all-to-all-start.1 = ((f32[64,1,128]{2,1,0:T(1,128)}), f32[64,1,128]{2,1,0:T(1,128)S(1)}, u32[]{:S(2)}, u32[]{:S(2)}) async-start(f32[64,1,128]{2,1,0:T(1,128)} %reshape.77), calls=%async_computation.1 | async-start | bytes 65536 | tf_op jit(solution)/shard_map/all_to_all | solution.py:16
